TPU v7x, 32 devices: a whole 2x2x4 slice. The times are simulated.
32 devices in a mesh: section: 4 (over x, core), head: 8 (over z, y).
Axes of the slice: x: 2, y: 2, z: 4, core: 2. Of those that a mesh axis runs over, the one named last changes fastest.
Arguments:
- hidden: float32 [4, 32, 7168], P(None, 'section'), may hold values from -6 to 6
- norm_gain: float32 [7168], replicated, may hold values from 0.5 to 1.5
- router: bfloat16 [7168, 8], replicated, may hold values from -0.0625 to 0.0625
- key_value_weight: bfloat16 [7168, 256], replicated, may hold values from -0.0625 to 0.0625
- query_master: float32 [7168, 1024], P('section', 'head'), may hold values from -0.0625 to 0.0625
- output_master: float32 [7168, 1024], P('section', 'head'), may hold values from -1 to 1
- key_value_cache: bfloat16 [32, 256, 256], P('section', 'head'), may hold values from -480 to 480
- lengths: int32 [32], P('section'), may hold values from 64 to 256
- routes: int32 [4, 32, 4], P(None, 'section'), may hold values from 0 to 7, all different within a row
Outputs:
- handed_on: float32 [4, 32, 7168], P(None, 'section', 'head')
All inputs are finite; a program needn't handle non-finite values.
Results may differ from a plain program's by a relative error of at most 0.012.
The roundings to bfloat16 on the way count: a program that leaves them out, or rounds other values in their place, can miss the bound.
Values may be sent and summed in bfloat16 or wider, within the bound.
No kernel may reach another device: no remote copies, remote signals or barrier semaphores. Data moves between devices by JAX's collectives and lax.ppermute only.
A program may use at most 64 MiB of HBM per device.

v0:
```python
import math
import jax
import jax.numpy as jnp
from jax import lax
from jax.sharding import PartitionSpec as P


def from_behind(value, axis, steps):
    count = lax.axis_size(axis)
    pairs = [(source, (source + steps) % count) for source in range(count)]
    return lax.ppermute(value, axis, pairs)


def body(
    hidden,
    norm_gain,
    router,
    key_value_weight,
    query_master,
    output_master,
    key_value_cache,
    lengths,
    routes,
):
    step_count, row_count, model_width = hidden.shape
    head_dim = key_value_weight.shape[1] // 2
    experts = router.shape[1]
    own_expert = lax.axis_index("head")
    query_piece = query_master.astype(jnp.bfloat16)
    output_piece = output_master.astype(jnp.bfloat16)
    query_weight, output_weight = (
        lax.all_gather(query_piece, "section", axis=0, tiled=True),
        lax.all_gather(output_piece, "section", axis=0, tiled=True),
    )
    mean_square = jnp.mean(hidden * hidden, axis=-1, keepdims=True)
    normed = (hidden * lax.rsqrt(mean_square + 1e-05) * norm_gain).astype(jnp.bfloat16)
    flat_rows = normed.reshape(step_count * row_count, model_width)
    logits = jnp.dot(flat_rows, router, preferred_element_type=jnp.float32).reshape(
        step_count, row_count, experts
    )
    expert_ids = jnp.arange(experts)
    chosen = jnp.sum((routes[..., None] == expert_ids).astype(jnp.float32), axis=2)
    picked = jax.nn.sigmoid(logits) * chosen
    gate_values = picked / jnp.sum(picked, axis=-1, keepdims=True)
    fresh_pairs = jnp.dot(flat_rows, key_value_weight, preferred_element_type=jnp.float32).astype(
        jnp.bfloat16
    )
    fresh_pairs = fresh_pairs.reshape(step_count, row_count, 2 * head_dim)
    key_new = fresh_pairs[..., :head_dim]
    value_new = fresh_pairs[..., head_dim:]
    queries = jnp.dot(flat_rows, query_weight, preferred_element_type=jnp.float32).astype(
        jnp.bfloat16
    )
    queries = queries.reshape(step_count, row_count, head_dim)
    score_factor = 1.0 / math.sqrt(head_dim)
    step_order = jnp.arange(step_count)
    fresh_mask = (step_order[None, :] <= step_order[:, None])[:, None, :]
    fresh_scores = (
        jnp.einsum("srh,urh->sru", queries, key_new, preferred_element_type=jnp.float32)
        * score_factor
    )
    fresh_peak = jnp.max(jnp.where(fresh_mask, fresh_scores, -jnp.inf), axis=-1)
    gathered = lax.all_gather(key_value_cache, "head", axis=1, tiled=True)
    positions = jnp.arange(gathered.shape[1])
    cache_mask = (positions[None, :] < lengths[:, None])[None, :, :]
    cache_scores = (
        jnp.einsum(
            "srh,rph->srp", queries, gathered[..., :head_dim], preferred_element_type=jnp.float32
        )
        * score_factor
    )
    highest = jnp.maximum(
        jnp.max(jnp.where(cache_mask, cache_scores, -jnp.inf), axis=-1), fresh_peak
    )
    cache_weights = jnp.where(cache_mask, jnp.exp(cache_scores - highest[..., None]), 0.0)
    mixture = jnp.einsum(
        "srp,rph->srh", cache_weights, gathered[..., head_dim:], preferred_element_type=jnp.float32
    )
    denominator = jnp.sum(cache_weights, axis=-1)
    fresh_weights = jnp.where(fresh_mask, jnp.exp(fresh_scores - highest[..., None]), 0.0)
    mixture = mixture + jnp.einsum(
        "sru,urh->srh", fresh_weights, value_new, preferred_element_type=jnp.float32
    )
    denominator = denominator + jnp.sum(fresh_weights, axis=-1)
    attended = (mixture / denominator[..., None]).astype(jnp.bfloat16)
    share_width = model_width // lax.axis_size("head")
    feature_slice = lax.all_to_all(output_weight, "head", split_axis=0, concat_axis=1, tiled=True)
    feature_slice = feature_slice.reshape(share_width, experts, head_dim)
    all_attended = lax.all_gather(attended[:, :, None, :], "head", axis=2, tiled=True)
    all_attended = all_attended.reshape(step_count * row_count, experts, head_dim)
    per_expert = jnp.einsum(
        "neh,feh->nef", all_attended, feature_slice, preferred_element_type=jnp.float32
    )
    gates_flat = gate_values.reshape(step_count * row_count, experts)
    summed = jnp.sum(gates_flat[..., None] * per_expert, axis=1)
    summed = summed.reshape(step_count, row_count, share_width)
    own_columns = lax.dynamic_slice_in_dim(hidden, own_expert * share_width, share_width, 2)
    result = own_columns + summed
    return from_behind(result, "section", 1)


def solution(mesh):
    return jax.shard_map(
        body,
        mesh=mesh,
        in_specs=(
            P(None, "section", None),
            P(),
            P(),
            P(),
            P("section", "head"),
            P("section", "head"),
            P("section", "head", None),
            P("section"),
            P(None, "section", None),
        ),
        out_specs=P(None, "section", "head"),
        check_vma=False,
    )
```

profile of v0, /device:TPU:0, one launch (start us, length us, event | category | flops | bytes accessed | tf_op | source)
XLA Modules:
  0.0 139.1 jit_solution(11316484669414816470)
XLA Ops:
  6.5 2.1 %convert_element_type.27 = bf16[1792,128]{1,0:T(8,128)(2,1)} convert(f32[1792,128]{1,0:T(8,128)} %param.14) | non-fusion elementwise | flops 229376 | bytes 1376256 | tf_op jit(solution)/shard_map/convert_element_type | solution.py:30
  8.8 0.8 convert_element_type.23
  9.7 0.7 all-gather.7.cloned.1.call-update
  10.4 0.2 multiply_reduce_fusion
  10.5 22.2 %all-gather.9.cloned.1.call-done = bf16[7168,128]{1,0:T(8,128)(2,1)} async-done(((bf16[1792,128]{1,0:T(8,128)(2,1)}), bf16[7168,128]{1,0:T(8,128)(2,1)}) %all-gather.9.cloned.1.call-update) | async-done | bytes 1835024 | tf_op jit(solution)/shard_map/all_gather | solution.py:33
  32.8 5.6 %all-to-all-start = ((bf16[8,896,128]{2,1,0:T(8,128)(2,1)}), bf16[8,896,128]{2,1,0:T(8,128)(2,1)S(1)}, u32[]{:S(2)}, u32[]{:S(2)}) async-start(bf16[8,896,128]{2,1,0:T(8,128)(2,1)} %bitcast.56), calls=%async_computation | async-start | bytes 3670016 | tf_op jit(solution)/shard_map/all_to_all | solution.py:87
  38.4 0.2 multiply_convert_fusion
  38.6 0.1 convert_reduce_fusion
  38.8 1.1 fusion.43
  39.9 0.1 mul.60
  40.0 0.1 iota_compare_fusion.1
  40.1 3.0 %fusion.12 = bf16[4,8,256]{2,1,0:T(8,128)(2,1)S(1)} fusion(bf16[7168,256]{1,0:T(8,128)(2,1)} %param.12, bf16[4,8,7168]{2,1,0:T(8,128)(2,1)S(1)} %multiply_convert_fusion), kind=kOutput, calls=%fused_computation.8 | convolution fusion | flops 117448704 | bytes 4145152 | tf_op jit(solution)/shard_map/dot_general | solution.py:45
  43.1 12.3 %all-gather.5.cloned.1.call-done = bf16[7168,128]{1,0:T(8,128)(2,1)} async-done(((bf16[1792,128]{1,0:T(8,128)(2,1)}), bf16[7168,128]{1,0:T(8,128)(2,1)}) %all-gather.5.cloned.1.call-update) | async-done | bytes 1835024 | tf_op jit(solution)/shard_map/all_gather | solution.py:32
  55.4 1.9 %fusion.21 = bf16[4,8,128]{2,1,0:T(8,128)(2,1)S(1)} fusion(bf16[7168,128]{1,0:T(8,128)(2,1)} %all-gather.5.cloned.1.call-done, bf16[4,8,7168]{2,1,0:T(8,128)(2,1)S(1)} %multiply_convert_fusion), kind=kOutput, calls=%fused_computation.22 | convolution fusion | flops 58724352 | bytes 2301952 | tf_op jit(solution)/shard_map/dot_general | solution.py:51
  57.3 0.1 select_reduce_fusion.1
  57.5 47.6 %all-gather.7.cloned.1.call-done = bf16[8,256,256]{2,1,0:T(8,128)(2,1)} async-done(((bf16[8,32,256]{2,1,0:T(8,128)(2,1)}), bf16[8,256,256]{2,1,0:T(8,128)(2,1)}) %all-gather.7.cloned.1.call-update) | async-done | bytes 1048592 | tf_op jit(solution)/shard_map/all_gather | solution.py:63
  105.1 1.4 select_reduce_fusion
  106.5 0.2 fusion.28
  106.7 1.3 convolution_bitcast_fusion.1
  108.0 0.2 fusion.20
  108.2 18.6 %all-gather = bf16[4,8,1024]{2,0,1:T(4,128)(2,1)S(1)} all-gather(bf16[4,8,128]{2,0,1:T(4,128)(2,1)S(1)} %fusion.20), channel_id=2, replica_groups=mesh['section'=4,'head'=8] {'head'}, dimensions={2}, use_global_device_ids=true | all-gather | bytes 73728 | tf_op jit(solution)/shard_map/all_gather | solution.py:89
  126.9 0.7 fusion.8
  127.7 4.2 %collective-permute-done = f32[4,8,896]{2,1,0:T(8,128)S(1)} collective-permute-done((f32[4,8,896]{2,1,0:T(8,128)S(1)}, f32[4,8,896]{2,1,0:T(8,128)S(1)}, u32[]{:S(2)}, u32[]{:S(2)}) %collective-permute-start) | collective-permute-done | bytes 114720 | tf_op jit(solution)/shard_map/ppermute | solution.py:11
  131.9 0.6 copy.57
  (31 shorter events, 0.4 us)
Async XLA Ops:
  6.5 32.2 %copy-start = (bf16[7168,8]{0,1:T(8,128)(2,1)S(1)}, bf16[7168,8]{0,1:T(8,128)(2,1)}, u32[]{:S(2)}) copy-start(bf16[7168,8]{0,1:T(8,128)(2,1)} %param.11) | copy-start | bytes 344068
  6.5 2.2 %copy-start.2 = (f32[1792,128]{1,0:T(8,128)S(1)}, f32[1792,128]{1,0:T(8,128)}, u32[]{:S(2)}) copy-start(f32[1792,128]{1,0:T(8,128)} %param.13) | copy-start | bytes 2752516
  6.5 3.8 %copy-start.1 = (f32[4,8,7168]{2,1,0:T(8,128)S(1)}, f32[4,8,7168]{2,1,0:T(8,128)}, u32[]{:S(2)}) copy-start(f32[4,8,7168]{2,1,0:T(8,128)} %param.9) | copy-start | bytes 2752516
  6.5 26.2 %all-gather.9.cloned.1.call-start = ((), (), s32[]{:S(2)}) async-start(), calls=%async_computation.3 | async-start | bytes 2293760 | tf_op jit(solution)/shard_map/all_gather | solution.py:33
  8.7 46.7 %all-gather.5.cloned.1.call-start = ((), (), s32[]{:S(2)}) async-start(), calls=%async_computation.1 | async-start | bytes 2293760 | tf_op jit(solution)/shard_map/all_gather | solution.py:32
  9.6 95.5 %all-gather.7.cloned.1.call-start = ((), (), s32[]{:S(2)}) async-start(), calls=%async_computation.2 | async-start | bytes 1179648 | tf_op jit(solution)/shard_map/all_gather | solution.py:63
  32.7 5.7 %copy-start.3 = (f32[7168]{0:T(1024)S(1)}, f32[7168]{0:T(1024)}, u32[]{:S(2)}) copy-start(f32[7168]{0:T(1024)} %param.10) | copy-start | bytes 86020
  32.8 5.8 %copy-start.4 = (s32[4,8,4]{1,2,0:T(4,128)S(1)}, s32[4,8,4]{1,2,0:T(4,128)}, u32[]{:S(2)}) copy-start(s32[4,8,4]{1,2,0:T(4,128)} %param.17) | copy-start | bytes 1540
  32.8 94.1 %all-to-all-start = ((bf16[8,896,128]{2,1,0:T(8,128)(2,1)}), bf16[8,896,128]{2,1,0:T(8,128)(2,1)S(1)}, u32[]{:S(2)}, u32[]{:S(2)}) async-start(bf16[8,896,128]{2,1,0:T(8,128)(2,1)} %bitcast.56), calls=%async_computation | async-start | bytes 3670016 | tf_op jit(solution)/shard_map/all_to_all | solution.py:87
  38.4 1.6 %copy-start.5 = (s32[8]{0:T(128)S(1)}, s32[8]{0:T(128)}, u32[]{:S(2)}) copy-start(s32[8]{0:T(128)} %param.16) | copy-start | bytes 100
  127.6 4.3 %collective-permute-start = (f32[4,8,896]{2,1,0:T(8,128)S(1)}, f32[4,8,896]{2,1,0:T(8,128)S(1)}, u32[]{:S(2)}, u32[]{:S(2)}) collective-permute-start(f32[4,8,896]{2,1,0:T(8,128)S(1)} %bitcast_add_fusion), channel_id=1, source_target_pairs={{0,8},{8,16},{16,24},{24,0},{1,9},{9,17},{17,25},{25,1},{2,10},{10... | collective-permute-start | bytes 344072 | tf_op jit(solution)/shard_map/ppermute | solution.py:11
Sparse Core Ops, SparseCore 0:
  8.9 23.8 all-gather.8
  34.3 21.0 all-gather.4
  57.6 47.4 all-gather.6
where the time goes:
time: 140 us; the launch traced here: 139 us
  waiting for transfers between devices  87.1 us (62%)
  blocking collectives  18.6 us (13%)
  between operations  13.3 us (10%)
  matrix products  9.74 us (7%)
  starting transfers between devices  5.79 us (4%)
  other arithmetic  3.71 us (3%)
    all_gather x1, waiting for transfers between devices, body(): gathered = lax.all_gather(key_value_cache, 'head', axis=1, tiled=True)  47.6 us
    all_gather x1, waiting for transfers between devices, body(): lax.all_gather(output_piece, 'section', axis=0, tiled=True)  22.2 us
    all_gather x1, blocking collectives, body(): lax.all_gather(attended[:, :, None, :], 'head', axis=2, tiled=True)  18.6 us
    all_gather x1, waiting for transfers between devices, body(): lax.all_gather(query_piece, 'section', axis=0, tiled=True)  12.3 us
    all_to_all x1, starting transfers between devices, body(): lax.all_to_all(output_weight, 'head', split_axis=0, concat_axis=1, tiled=...  5.65 us
    ppermute x1, waiting for transfers between devices, from_behind(): return lax.ppermute(value, axis, pairs)  4.2 us
    dot_general x1, matrix products, body(): jnp.dot(flat_rows, key_value_weight, preferred_element_type=jnp.float32)  2.97 us
  transfers between devices with their start and end apart: 5, of which 4 were waited for; matrix products, arithmetic and copies ran while one was open for 8% of the time, Pallas kernels for 0%

commit v1 on v0

--- a/solution.py
+++ b/solution.py
@@ -3,6 +3,17 @@
 import jax.numpy as jnp
 from jax import lax
 from jax.sharding import PartitionSpec as P
+
+
+def turned_line(value, axis, along):
+    size = lax.axis_size(axis)
+    right = [(i, (i + 1) % size) for i in range(size)]
+    parts = [value]
+    for far in range(1, size):
+        parts = [lax.ppermute(parts[0], axis, right), *parts]
+    whole = jnp.concatenate(parts, axis=along)
+    shift = (lax.axis_index(axis) + 1) * parts[-1].shape[along]
+    return jnp.roll(whole, shift, axis=along)
 
 
 def from_behind(value, axis, steps):
@@ -60,7 +71,7 @@
         * score_factor
     )
     fresh_peak = jnp.max(jnp.where(fresh_mask, fresh_scores, -jnp.inf), axis=-1)
-    gathered = lax.all_gather(key_value_cache, "head", axis=1, tiled=True)
+    gathered = turned_line(key_value_cache, "head", 1)
     positions = jnp.arange(gathered.shape[1])
     cache_mask = (positions[None, :] < lengths[:, None])[None, :, :]
     cache_scores = (

time: 140 us -> 124 us (0.89)
  waiting for transfers between devices: 87.1 us -> 47.9 us
  local copies, waits for them, and re-layouts: 0.87 us -> 20.4 us
  starting transfers between devices: 5.79 us -> 9.33 us
    all_gather x1 -> x0, waiting for transfers between devices: 47.6 us -> none  [body(): gathered = lax.all_gather(key_value_cache, 'head', axis=1, tiled=True)]
    ppermute x0 -> x7, waiting for transfers between devices: none -> 43.7 us  [turned_line(): parts = [lax.ppermute(parts[0], axis, right), *parts]]
    all_gather x1, waiting for transfers between devices: 22.2 us -> 0.01 us  [body(): lax.all_gather(output_piece, 'section', axis=0, tiled=True)]
    unnamed x14 -> x51, local copies, waits for them, and re-layouts: 0.68 us -> 19.6 us
    all_gather x1, waiting for transfers between devices: 12.3 us -> 0.01 us  [body(): lax.all_gather(query_piece, 'section', axis=0, tiled=True)]
    ppermute x0 -> x7, starting transfers between devices: none -> 3.06 us  [turned_line(): parts = [lax.ppermute(parts[0], axis, right), *parts]]
  transfers between devices with their start and end apart: 5 -> 11, of which waited for: 4 -> 8; matrix products, arithmetic and copies ran while one was open for 8% -> 24% of each run, Pallas kernels for 0% -> 0%
where the time goes in v1:
time: 124 us; the launch traced here: 123 us
  waiting for transfers between devices  47.9 us (39%)
  local copies, waits for them, and re-layouts  20.4 us (16%)
  blocking collectives  18.5 us (15%)
  between operations  13.6 us (11%)
  matrix products  9.6 us (8%)
  starting transfers between devices  9.33 us (8%)
  other arithmetic  3.68 us (3%)
    ppermute x7, waiting for transfers between devices, turned_line(): parts = [lax.ppermute(parts[0], axis, right), *parts]  43.7 us
    unnamed x51, local copies, waits for them, and re-layouts  19.6 us
    all_gather x1, blocking collectives, body(): lax.all_gather(attended[:, :, None, :], 'head', axis=2, tiled=True)  18.5 us
    all_to_all x1, starting transfers between devices, body(): lax.all_to_all(output_weight, 'head', split_axis=0, concat_axis=1, tiled=...  6.14 us
    ppermute x1, waiting for transfers between devices, from_behind(): return lax.ppermute(value, axis, pairs)  4.2 us
    ppermute x7, starting transfers between devices, turned_line(): parts = [lax.ppermute(parts[0], axis, right), *parts]  3.06 us
    dot_general x1, matrix products, body(): jnp.dot(flat_rows, key_value_weight, preferred_element_type=jnp.float32)  2.83 us
  transfers between devices with their start and end apart: 11, of which 8 were waited for; matrix products, arithmetic and copies ran while one was open for 24% of the time, Pallas kernels for 0%

profile of v1, /device:TPU:0, one launch (start us, length us, event | category | flops | bytes accessed | tf_op | source)
XLA Modules:
  0.0 123.1 jit_solution(9709237775303472976)
XLA Ops:
  6.6 2.1 %convert_element_type.27 = bf16[1792,128]{1,0:T(8,128)(2,1)} convert(f32[1792,128]{1,0:T(8,128)} %param.14) | non-fusion elementwise | flops 229376 | bytes 1376256 | tf_op jit(solution)/shard_map/convert_element_type | solution.py:41
  8.8 3.0 %collective-permute-start = (bf16[8,32,256]{2,1,0:T(8,128)(2,1)}, bf16[8,32,256]{2,1,0:T(8,128)(2,1)S(1)}, u32[]{:S(2)}, u32[]{:S(2)}) collective-permute-start(bf16[8,32,256]{2,1,0:T(8,128)(2,1)} %param.15), channel_id=1, source_target_pairs={{0,1},{1,2},{2,3},{3,4},{4,5},{5,6},{6,7},{7,0},{8,9},{9,10},{10,1... | collective-permute-start | bytes 393224 | tf_op jit(solution)/shard_map/ppermute | solution.py:13
  12.9 5.7 %collective-permute-done = bf16[8,32,256]{2,1,0:T(8,128)(2,1)S(1)} collective-permute-done((bf16[8,32,256]{2,1,0:T(8,128)(2,1)}, bf16[8,32,256]{2,1,0:T(8,128)(2,1)S(1)}, u32[]{:S(2)}, u32[]{:S(2)}) %collective-permute-start) | collective-permute-done | bytes 131104 | tf_op jit(solution)/shard_map/ppermute | solution.py:13
  18.8 7.5 %collective-permute-done.1 = bf16[8,32,256]{2,1,0:T(8,128)(2,1)S(1)} collective-permute-done((bf16[8,32,256]{2,1,0:T(8,128)(2,1)S(1)}, bf16[8,32,256]{2,1,0:T(8,128)(2,1)S(1)}, u32[]{:S(2)}, u32[]{:S(2)}) %collective-permute-start.1) | collective-permute-done | bytes 131104 | tf_op jit(solution)/shard_map/ppermute | solution.py:13
  26.3 2.8 %fusion.12 = bf16[4,8,256]{2,1,0:T(8,128)(2,1)S(1)} fusion(bf16[7168,256]{1,0:T(8,128)(2,1)} %param.12, bf16[4,8,7168]{2,1,0:T(8,128)(2,1)S(1)} %multiply_convert_fusion), kind=kOutput, calls=%fused_computation.8 | convolution fusion | flops 117448704 | bytes 4145152 | tf_op jit(solution)/shard_map/dot_general | solution.py:56
  29.3 4.6 %collective-permute-done.2 = bf16[8,32,256]{2,1,0:T(8,128)(2,1)S(1)} collective-permute-done((bf16[8,32,256]{2,1,0:T(8,128)(2,1)S(1)}, bf16[8,32,256]{2,1,0:T(8,128)(2,1)S(1)}, u32[]{:S(2)}, u32[]{:S(2)}) %collective-permute-start.2) | collective-permute-done | bytes 131104 | tf_op jit(solution)/shard_map/ppermute | solution.py:13
  35.1 6.5 %collective-permute-done.3 = bf16[8,32,256]{2,1,0:T(8,128)(2,1)S(1)} collective-permute-done((bf16[8,32,256]{2,1,0:T(8,128)(2,1)S(1)}, bf16[8,32,256]{2,1,0:T(8,128)(2,1)S(1)}, u32[]{:S(2)}, u32[]{:S(2)}) %collective-permute-start.3) | collective-permute-done | bytes 131104 | tf_op jit(solution)/shard_map/ppermute | solution.py:13
  41.6 7.7 %collective-permute-done.4 = bf16[8,32,256]{2,1,0:T(8,128)(2,1)S(1)} collective-permute-done((bf16[8,32,256]{2,1,0:T(8,128)(2,1)S(1)}, bf16[8,32,256]{2,1,0:T(8,128)(2,1)S(1)}, u32[]{:S(2)}, u32[]{:S(2)}) %collective-permute-start.4) | collective-permute-done | bytes 131104 | tf_op jit(solution)/shard_map/ppermute | solution.py:13
  49.9 8.6 %collective-permute-done.5 = bf16[8,32,256]{2,1,0:T(8,128)(2,1)} collective-permute-done((bf16[8,32,256]{2,1,0:T(8,128)(2,1)S(1)}, bf16[8,32,256]{2,1,0:T(8,128)(2,1)}, u32[]{:S(2)}, u32[]{:S(2)}) %collective-permute-start.5) | collective-permute-done | bytes 131104 | tf_op jit(solution)/shard_map/ppermute | solution.py:13
  58.8 6.1 %all-to-all-start = ((bf16[8,896,128]{2,1,0:T(8,128)(2,1)}), bf16[8,896,128]{2,1,0:T(8,128)(2,1)S(1)}, u32[]{:S(2)}, u32[]{:S(2)}) async-start(bf16[8,896,128]{2,1,0:T(8,128)(2,1)} %bitcast.52), calls=%async_computation | async-start | bytes 3670016 | tf_op jit(solution)/shard_map/all_to_all | solution.py:98
  64.9 3.1 %collective-permute-done.6 = bf16[8,32,256]{2,1,0:T(8,128)(2,1)} collective-permute-done((bf16[8,32,256]{2,1,0:T(8,128)(2,1)}, bf16[8,32,256]{2,1,0:T(8,128)(2,1)}, u32[]{:S(2)}, u32[]{:S(2)}) %collective-permute-start.6) | collective-permute-done | bytes 131104 | tf_op jit(solution)/shard_map/ppermute | solution.py:13
  68.0 1.6 %constant_dynamic-update-slice_fusion.15 = bf16[8,512,256]{2,1,0:T(8,128)(2,1)} fusion(bf16[8,32,256]{2,1,0:T(8,128)(2,1)} %collective-permute-done.6), kind=kLoop, calls=%fused_computation.49 | loop fusion | bytes 262144
  69.6 1.6 %constant_dynamic-update-slice_fusion.14 = bf16[8,512,256]{2,1,0:T(8,128)(2,1)} fusion(bf16[8,512,256]{2,1,0:T(8,128)(2,1)} %constant_dynamic-update-slice_fusion.15, bf16[8,32,256]{2,1,0:T(8,128)(2,1)} %collective-permute-done.5), kind=kLoop, calls=%fused_computation.48 | loop fusion | bytes 262144
  71.2 1.6 %constant_dynamic-update-slice_fusion.13 = bf16[8,512,256]{2,1,0:T(8,128)(2,1)} fusion(bf16[8,512,256]{2,1,0:T(8,128)(2,1)} %constant_dynamic-update-slice_fusion.14, bf16[8,32,256]{2,1,0:T(8,128)(2,1)} %copy-done.12), kind=kLoop, calls=%fused_computation.47 | loop fusion | bytes 262144
  72.7 1.6 %constant_dynamic-update-slice_fusion.12 = bf16[8,512,256]{2,1,0:T(8,128)(2,1)} fusion(bf16[8,512,256]{2,1,0:T(8,128)(2,1)} %constant_dynamic-update-slice_fusion.13, bf16[8,32,256]{2,1,0:T(8,128)(2,1)} %copy-done.10), kind=kLoop, calls=%fused_computation.46 | loop fusion | bytes 262144
  74.3 1.6 %constant_dynamic-update-slice_fusion.11 = bf16[8,512,256]{2,1,0:T(8,128)(2,1)} fusion(bf16[8,512,256]{2,1,0:T(8,128)(2,1)} %constant_dynamic-update-slice_fusion.12, bf16[8,32,256]{2,1,0:T(8,128)(2,1)} %copy-done.8), kind=kLoop, calls=%fused_computation.45 | loop fusion | bytes 262144
  75.9 1.6 %constant_dynamic-update-slice_fusion.10 = bf16[8,512,256]{2,1,0:T(8,128)(2,1)} fusion(bf16[8,512,256]{2,1,0:T(8,128)(2,1)} %constant_dynamic-update-slice_fusion.11, bf16[8,32,256]{2,1,0:T(8,128)(2,1)} %copy-done.6), kind=kLoop, calls=%fused_computation.44 | loop fusion | bytes 262144
  77.4 1.6 %constant_dynamic-update-slice_fusion.9 = bf16[8,512,256]{2,1,0:T(8,128)(2,1)} fusion(bf16[8,512,256]{2,1,0:T(8,128)(2,1)} %constant_dynamic-update-slice_fusion.10, bf16[8,32,256]{2,1,0:T(8,128)(2,1)} %copy-done.4), kind=kLoop, calls=%fused_computation.43 | loop fusion | bytes 262144
  79.7 1.6 %constant_dynamic-update-slice_fusion.7 = bf16[8,512,256]{2,1,0:T(8,128)(2,1)} fusion(bf16[8,512,256]{2,1,0:T(8,128)(2,1)} %constant_dynamic-update-slice_fusion.8, bf16[8,32,256]{2,1,0:T(8,128)(2,1)} %collective-permute-done.6), kind=kLoop, calls=%fused_computation.41 | loop fusion | bytes 262144
  81.3 1.6 %constant_dynamic-update-slice_fusion.6 = bf16[8,512,256]{2,1,0:T(8,128)(2,1)} fusion(bf16[8,512,256]{2,1,0:T(8,128)(2,1)} %constant_dynamic-update-slice_fusion.7, bf16[8,32,256]{2,1,0:T(8,128)(2,1)} %collective-permute-done.5), kind=kLoop, calls=%fused_computation.40 | loop fusion | bytes 262144
  86.9 1.9 %fusion.21 = bf16[4,8,128]{2,1,0:T(8,128)(2,1)S(1)} fusion(bf16[7168,128]{1,0:T(8,128)(2,1)} %all-gather.4.cloned.1.call-done, bf16[4,8,7168]{2,1,0:T(8,128)(2,1)S(1)} %multiply_convert_fusion), kind=kOutput, calls=%fused_computation.21 | convolution fusion | flops 58724352 | bytes 2301952 | tf_op jit(solution)/shard_map/dot_general | solution.py:62
  88.9 1.4 %select_reduce_fusion = (f32[4,8]{0,1:T(8,128)S(1)}, f32[4,8,256]{2,0,1:T(4,128)S(1)}) fusion(pred[8,256]{1,0:T(8,128)(4,1)S(1)} %iota_compare_fusion.1, bf16[4,8,128]{2,1,0:T(8,128)(2,1)S(1)} %fusion.21, bf16[8,512,256]{2,1,0:T(8,128)(2,1)} %constant_dynamic-update-slice_fusion, s32[]{:T(128)S(6)} %select_n.32), kind=kOutput, calls=%fused_computation.51 | convolution fusion | flops 2121696 | bytes 567428 | tf_op jit(solution)/shard_map/srh,rph->srp/dot_general | solution.py:78
  92.0 18.5 %all-gather = bf16[4,8,1024]{2,0,1:T(4,128)(2,1)S(1)} all-gather(bf16[4,8,128]{2,0,1:T(4,128)(2,1)S(1)} %fusion.20), channel_id=2, replica_groups=mesh['section'=4,'head'=8] {'head'}, dimensions={2}, use_global_device_ids=true | all-gather | bytes 73728 | tf_op jit(solution)/shard_map/all_gather | solution.py:100
  111.4 4.2 %collective-permute-done.7 = f32[4,8,896]{2,1,0:T(8,128)S(1)} collective-permute-done((f32[4,8,896]{2,1,0:T(8,128)S(1)}, f32[4,8,896]{2,1,0:T(8,128)S(1)}, u32[]{:S(2)}, u32[]{:S(2)}) %collective-permute-start.7) | collective-permute-done | bytes 114720 | tf_op jit(solution)/shard_map/ppermute | solution.py:22
  (80 shorter events, 11.5 us)
Async XLA Ops:
  6.5 27.4 %copy-start = (bf16[7168,8]{0,1:T(8,128)(2,1)S(1)}, bf16[7168,8]{0,1:T(8,128)(2,1)}, u32[]{:S(2)}) copy-start(bf16[7168,8]{0,1:T(8,128)(2,1)} %param.11) | copy-start | bytes 344068
  6.5 12.1 %copy-start.14 = (f32[7168]{0:T(1024)S(1)}, f32[7168]{0:T(1024)}, u32[]{:S(2)}) copy-start(f32[7168]{0:T(1024)} %param.10) | copy-start | bytes 86020
  6.5 52.2 %all-gather.6.cloned.1.call-start = ((), (), s32[]{:S(2)}) async-start(), calls=%async_computation.2 | async-start | bytes 2293760 | tf_op jit(solution)/shard_map/all_gather | solution.py:44
  8.7 78.1 %all-gather.4.cloned.1.call-start = ((), (), s32[]{:S(2)}) async-start(), calls=%async_computation.1 | async-start | bytes 2293760 | tf_op jit(solution)/shard_map/all_gather | solution.py:43
  8.8 9.8 %collective-permute-start = (bf16[8,32,256]{2,1,0:T(8,128)(2,1)}, bf16[8,32,256]{2,1,0:T(8,128)(2,1)S(1)}, u32[]{:S(2)}, u32[]{:S(2)}) collective-permute-start(bf16[8,32,256]{2,1,0:T(8,128)(2,1)} %param.15), channel_id=1, source_target_pairs={{0,1},{1,2},{2,3},{3,4},{4,5},{5,6},{6,7},{7,0},{8,9},{9,10},{10,1... | collective-permute-start | bytes 393224 | tf_op jit(solution)/shard_map/ppermute | solution.py:13
  18.6 10.5 %copy-start.4 = (bf16[8,32,256]{2,1,0:T(8,128)(2,1)}, bf16[8,32,256]{2,1,0:T(8,128)(2,1)S(1)}, u32[]{:S(2)}) copy-start(bf16[8,32,256]{2,1,0:T(8,128)(2,1)S(1)} %collective-permute-done) | copy-start | bytes 393220
  18.6 7.7 %collective-permute-start.1 = (bf16[8,32,256]{2,1,0:T(8,128)(2,1)S(1)}, bf16[8,32,256]{2,1,0:T(8,128)(2,1)S(1)}, u32[]{:S(2)}, u32[]{:S(2)}) collective-permute-start(bf16[8,32,256]{2,1,0:T(8,128)(2,1)S(1)} %collective-permute-done), channel_id=1, source_target_pairs={{0,1},{1,2},{2,3},{3,4},{4,5},{5,6},{6,7},{7,0},{8,9},{9,10},{10,1... | collective-permute-start | bytes 393224 | tf_op jit(solution)/shard_map/ppermute | solution.py:13
  18.8 10.4 %copy-start.15 = (s32[4,8,4]{1,2,0:T(4,128)S(1)}, s32[4,8,4]{1,2,0:T(4,128)}, u32[]{:S(2)}) copy-start(s32[4,8,4]{1,2,0:T(4,128)} %param.17) | copy-start | bytes 1540
  18.8 39.8 %copy-start.16 = (s32[8]{0:T(128)S(1)}, s32[8]{0:T(128)}, u32[]{:S(2)}) copy-start(s32[8]{0:T(128)} %param.16) | copy-start | bytes 100
  26.3 7.7 %collective-permute-start.2 = (bf16[8,32,256]{2,1,0:T(8,128)(2,1)S(1)}, bf16[8,32,256]{2,1,0:T(8,128)(2,1)S(1)}, u32[]{:S(2)}, u32[]{:S(2)}) collective-permute-start(bf16[8,32,256]{2,1,0:T(8,128)(2,1)S(1)} %collective-permute-done.1), channel_id=1, source_target_pairs={{0,1},{1,2},{2,3},{3,4},{4,5},{5,6},{6,7},{7,0},{8,9},{9,10},{10,1... | collective-permute-start | bytes 393224 | tf_op jit(solution)/shard_map/ppermute | solution.py:13
  33.9 24.8 %copy-start.8 = (bf16[8,32,256]{2,1,0:T(8,128)(2,1)}, bf16[8,32,256]{2,1,0:T(8,128)(2,1)S(1)}, u32[]{:S(2)}) copy-start(bf16[8,32,256]{2,1,0:T(8,128)(2,1)S(1)} %collective-permute-done.2) | copy-start | bytes 393220
  33.9 7.7 %collective-permute-start.3 = (bf16[8,32,256]{2,1,0:T(8,128)(2,1)S(1)}, bf16[8,32,256]{2,1,0:T(8,128)(2,1)S(1)}, u32[]{:S(2)}, u32[]{:S(2)}) collective-permute-start(bf16[8,32,256]{2,1,0:T(8,128)(2,1)S(1)} %collective-permute-done.2), channel_id=1, source_target_pairs={{0,1},{1,2},{2,3},{3,4},{4,5},{5,6},{6,7},{7,0},{8,9},{9,10},{10,1... | collective-permute-start | bytes 393224 | tf_op jit(solution)/shard_map/ppermute | solution.py:13
  41.6 17.2 %copy-start.10 = (bf16[8,32,256]{2,1,0:T(8,128)(2,1)}, bf16[8,32,256]{2,1,0:T(8,128)(2,1)S(1)}, u32[]{:S(2)}) copy-start(bf16[8,32,256]{2,1,0:T(8,128)(2,1)S(1)} %collective-permute-done.3) | copy-start | bytes 393220
  41.6 7.7 %collective-permute-start.4 = (bf16[8,32,256]{2,1,0:T(8,128)(2,1)S(1)}, bf16[8,32,256]{2,1,0:T(8,128)(2,1)S(1)}, u32[]{:S(2)}, u32[]{:S(2)}) collective-permute-start(bf16[8,32,256]{2,1,0:T(8,128)(2,1)S(1)} %collective-permute-done.3), channel_id=1, source_target_pairs={{0,1},{1,2},{2,3},{3,4},{4,5},{5,6},{6,7},{7,0},{8,9},{9,10},{10,1... | collective-permute-start | bytes 393224 | tf_op jit(solution)/shard_map/ppermute | solution.py:13
  49.9 8.6 %collective-permute-start.5 = (bf16[8,32,256]{2,1,0:T(8,128)(2,1)S(1)}, bf16[8,32,256]{2,1,0:T(8,128)(2,1)}, u32[]{:S(2)}, u32[]{:S(2)}) collective-permute-start(bf16[8,32,256]{2,1,0:T(8,128)(2,1)S(1)} %collective-permute-done.4), channel_id=1, source_target_pairs={{0,1},{1,2},{2,3},{3,4},{4,5},{5,6},{6,7},{7,0},{8,9},{9,10},{10,1... | collective-permute-start | bytes 393224 | tf_op jit(solution)/shard_map/ppermute | solution.py:13
  58.6 9.4 %collective-permute-start.6 = (bf16[8,32,256]{2,1,0:T(8,128)(2,1)}, bf16[8,32,256]{2,1,0:T(8,128)(2,1)}, u32[]{:S(2)}, u32[]{:S(2)}) collective-permute-start(bf16[8,32,256]{2,1,0:T(8,128)(2,1)} %collective-permute-done.5), channel_id=1, source_target_pairs={{0,1},{1,2},{2,3},{3,4},{4,5},{5,6},{6,7},{7,0},{8,9},{9,10},{10,1... | collective-permute-start | bytes 393224 | tf_op jit(solution)/shard_map/ppermute | solution.py:13
  58.7 20.3 %copy-start.3 = (bf16[8,32,256]{2,1,0:T(8,128)(2,1)S(1)}, bf16[8,32,256]{2,1,0:T(8,128)(2,1)}, u32[]{:S(2)}) copy-start(bf16[8,32,256]{2,1,0:T(8,128)(2,1)} %param.15) | copy-start | bytes 393220
  58.8 51.8 %all-to-all-start = ((bf16[8,896,128]{2,1,0:T(8,128)(2,1)}), bf16[8,896,128]{2,1,0:T(8,128)(2,1)S(1)}, u32[]{:S(2)}, u32[]{:S(2)}) async-start(bf16[8,896,128]{2,1,0:T(8,128)(2,1)} %bitcast.52), calls=%async_computation | async-start | bytes 3670016 | tf_op jit(solution)/shard_map/all_to_all | solution.py:98
  64.9 17.9 %copy-start.13 = (bf16[8,32,256]{2,1,0:T(8,128)(2,1)S(1)}, bf16[8,32,256]{2,1,0:T(8,128)(2,1)}, u32[]{:S(2)}) copy-start(bf16[8,32,256]{2,1,0:T(8,128)(2,1)} %copy-done.12) | copy-start | bytes 393220
  64.9 18.6 %copy-start.11 = (bf16[8,32,256]{2,1,0:T(8,128)(2,1)S(1)}, bf16[8,32,256]{2,1,0:T(8,128)(2,1)}, u32[]{:S(2)}) copy-start(bf16[8,32,256]{2,1,0:T(8,128)(2,1)} %copy-done.10) | copy-start | bytes 393220
  64.9 19.3 %copy-start.9 = (bf16[8,32,256]{2,1,0:T(8,128)(2,1)S(1)}, bf16[8,32,256]{2,1,0:T(8,128)(2,1)}, u32[]{:S(2)}) copy-start(bf16[8,32,256]{2,1,0:T(8,128)(2,1)} %copy-done.8) | copy-start | bytes 393220
  64.9 19.9 %copy-start.7 = (bf16[8,32,256]{2,1,0:T(8,128)(2,1)S(1)}, bf16[8,32,256]{2,1,0:T(8,128)(2,1)}, u32[]{:S(2)}) copy-start(bf16[8,32,256]{2,1,0:T(8,128)(2,1)} %copy-done.6) | copy-start | bytes 393220
  64.9 20.6 %copy-start.5 = (bf16[8,32,256]{2,1,0:T(8,128)(2,1)S(1)}, bf16[8,32,256]{2,1,0:T(8,128)(2,1)}, u32[]{:S(2)}) copy-start(bf16[8,32,256]{2,1,0:T(8,128)(2,1)} %copy-done.4) | copy-start | bytes 393220
  111.4 4.3 %collective-permute-start.7 = (f32[4,8,896]{2,1,0:T(8,128)S(1)}, f32[4,8,896]{2,1,0:T(8,128)S(1)}, u32[]{:S(2)}, u32[]{:S(2)}) collective-permute-start(f32[4,8,896]{2,1,0:T(8,128)S(1)} %bitcast_add_fusion), channel_id=1, source_target_pairs={{0,8},{8,16},{16,24},{24,0},{1,9},{9,17},{17,25},{25,1},{2,10},{10... | collective-permute-start | bytes 344072 | tf_op jit(solution)/shard_map/ppermute | solution.py:22
  (4 other events, 15.1 us)
Sparse Core Ops, SparseCore 0:
  8.9 23.8 all-gather.5
  34.3 21.0 all-gather.3
